TPU v7x, 32 devices: a whole 2x2x4 slice. The times are simulated.
32 devices in a mesh: replica: 4 (over x, core), fsdp: 8 (over z, y).
Axes of the slice: x: 2, y: 2, z: 4, core: 2. Of those that a mesh axis runs over, the one named last changes fastest.
Arguments:
- deltas: bfloat16 [4, 2, 2048, 16384], P('replica', None, 'fsdp'), may hold values from -3 to 3
- master: float32 [2, 2048, 16384], P(None, 'replica', 'fsdp'), may hold values from -3 to 3
- momentum: float32 [2, 2048, 16384], P(None, 'replica', 'fsdp'), may hold values from -2 to 2
Outputs:
- master_out: float32 [2, 2048, 16384], P(None, 'replica', 'fsdp')
- momentum_out: float32 [2, 2048, 16384], P(None, 'replica', 'fsdp')
- params_out: bfloat16 [2, 2048, 16384], P(None, 'fsdp')
All inputs are finite; a program needn't handle non-finite values.
Results may differ from a plain program's by a relative error of at most 0.008.
Values may be sent and summed in bfloat16 or wider, within the bound.
A program may use at most 128 MiB of HBM per device.

v0:
```python
import jax
import jax.numpy as jnp
from jax import lax
from jax.sharding import PartitionSpec as P


def on_device(deltas, master, momentum):
    local = deltas[0]
    groups = lax.axis_size("replica")
    moved = lax.all_to_all(local, "fsdp", split_axis=2, concat_axis=1, tiled=True)
    summed = lax.psum_scatter(
        moved.astype(jnp.float32).astype(jnp.bfloat16), "replica", scatter_dimension=1, tiled=True
    ).astype(jnp.float32)
    outer = summed / groups
    velocity = 0.9 * momentum + outer
    updated = master - 0.7 * (outer + 0.9 * velocity)
    rounded = updated.astype(jnp.bfloat16)
    copies = lax.all_gather(rounded, "replica", axis=1, tiled=True)
    spread = lax.all_to_all(copies, "fsdp", split_axis=1, concat_axis=2, tiled=True)
    return (updated, velocity, spread)


def solution(mesh):
    return jax.shard_map(
        on_device,
        mesh=mesh,
        in_specs=(
            P("replica", None, "fsdp", None),
            P(None, "replica", "fsdp"),
            P(None, "replica", "fsdp"),
        ),
        out_specs=(P(None, "replica", "fsdp"), P(None, "replica", "fsdp"), P(None, "fsdp", None)),
        check_vma=False,
    )
```

profile of v0, /device:TPU:0, one launch (start us, length us, event | category | flops | bytes accessed | tf_op | source)
XLA Modules:
  0.0 1325.4 jit_solution(8873194051052167290)
XLA Ops:
  7.2 0.0 all-reduce.3.cloned.1.call-start
  7.2 40.8 %copy.22 = bf16[1,2,256,16384]{2,1,3,0:T(2,128)(2,1)} copy(bf16[1,2,256,16384]{3,2,1,0:T(8,128)(2,1)} %param.3) | data formatting | bytes 33554432 | tf_op args[0]
  48.0 372.0 %all_to_all.36 = bf16[2,256,16384]{1,0,2:T(2,128)(2,1)} all-to-all(bf16[2,256,16384]{1,0,2:T(2,128)(2,1)} %bitcast.14), channel_id=1, replica_groups=mesh['replica'=4,'fsdp'=8] {'fsdp'}, dimensions={2} | all-to-all | bytes 33554432 | tf_op jit(solution)/shard_map/all_to_all | solution.py:10
  420.0 60.3 %copy.23 = bf16[2,8,256,2048]{3,0,2,1:T(2,128)(2,1)} copy(bf16[2,8,256,2048]{2,0,3,1:T(2,128)(2,1)} %bitcast.12) | data formatting | bytes 33554432 | tf_op jit(solution)/shard_map/all_to_all | solution.py:10
  480.3 0.0 copy-start
  480.3 0.0 all-reduce.3.cloned.1.call-update
  480.3 0.0 all-gather.2.cloned.1.call-start
  480.4 0.6 copy-done
  481.0 0.6 dynamic-slice
  482.2 285.7 %all-reduce.3.cloned.1.call-done = bf16[2,2048,2048]{2,0,1:T(2,128)(2,1)} async-done(((bf16[2,2048,2048]{2,0,1:T(2,128)(2,1)}), bf16[2,2048,2048]{2,0,1:T(2,128)(2,1)}) %all-reduce.3.cloned.1.call-update) | async-done | bytes 16777232
  767.9 5.1 constant_dynamic-slice_fusion
  773.0 13.9 %fusion = (bf16[2,512,2048]{2,1,0:T(8,128)(2,1)}, f32[2,512,2048]{2,1,0:T(8,128)}, f32[2,512,2048]{2,1,0:T(8,128)}) fusion(f32[2,512,2048]{2,1,0:T(8,128)} %param.4, bf16[2,512,2048]{2,0,1:T(2,128)(2,1)S(1)} %constant_dynamic-slice_fusion, f32[2,512,2048]{2,1,0:T(8,128)} %param.5), kind=kLoop, calls=%fused_computation.4 | loop fusion | flops 18874368 | bytes 41943040 | tf_op jit(solution)/shard_map/convert_element_type | solution.py:17
  786.9 8.4 copy.25
  795.3 0.0 all-gather.2.cloned.1.call-update
  795.3 106.1 %all-gather.2.cloned.1.call-done = bf16[2,2048,2048]{2,0,1:T(2,128)(2,1)} async-done(((bf16[2,512,2048]{2,0,1:T(2,128)(2,1)}), bf16[2,2048,2048]{2,0,1:T(2,128)(2,1)}) %all-gather.2.cloned.1.call-update) | async-done | bytes 16777232 | tf_op jit(solution)/shard_map/all_gather | solution.py:18
  901.4 368.7 %all_to_all.37 = bf16[2,2048,2048]{2,0,1:T(2,128)(2,1)S(1)} all-to-all(bf16[2,2048,2048]{2,0,1:T(2,128)(2,1)} %all-gather.2.cloned.1.call-done), channel_id=1, replica_groups=mesh['replica'=4,'fsdp'=8] {'fsdp'}, dimensions={1} | all-to-all | bytes 33554432 | tf_op jit(solution)/shard_map/all_to_all | solution.py:19
  1270.1 22.9 %copy.26 = bf16[2,256,8,2048]{3,2,1,0:T(8,128)(2,1)} copy(bf16[2,256,8,2048]{3,0,1,2:T(2,128)(2,1)S(1)} %bitcast.13) | data formatting | bytes 33554432 | tf_op jit(solution)/shard_map/all_to_all | solution.py:19
  1293.0 25.5 %all_to_all.33 = bf16[2,256,16384]{2,1,0:T(8,128)(2,1)} reshape(bf16[2,256,8,2048]{3,2,1,0:T(8,128)(2,1)} %copy.26) | data formatting | bytes 33554432 | tf_op jit(solution)/shard_map/all_to_all | solution.py:19
Async XLA Ops:
  7.2 760.7 %all-reduce.3.cloned.1.call-start = ((), (), s32[]{:S(2)}) async-start(), calls=%async_computation.3 | async-start | bytes 33554432
  480.3 0.7 copy-start
  480.3 421.1 %all-gather.2.cloned.1.call-start = ((), (), s32[]{:S(2)}) async-start(), calls=%async_computation.2 | async-start | bytes 20971520 | tf_op jit(solution)/shard_map/all_gather | solution.py:18
Sparse Core Ops, SparseCore 0:
  480.4 287.3 all-reduce.2
  795.5 105.9 all-gather.1
where the time goes:
time: 1330 us
  blocking collectives  741 us (56%)
  waiting for transfers between devices  392 us (29%)
  local copies, waits for them, and re-layouts  164 us (12%)
  between operations  14.7 us (1%)
  other arithmetic  13.9 us (1%)
    all_to_all x1, blocking collectives, on_device(): lax.all_to_all(local, 'fsdp', split_axis=2, concat_axis=1, tiled=True)  372 us
    all_to_all x1, blocking collectives, on_device(): lax.all_to_all(copies, 'fsdp', split_axis=1, concat_axis=2, tiled=True)  369 us
    unnamed x3, waiting for transfers between devices  286 us
    all_gather x1, waiting for transfers between devices, on_device(): copies = lax.all_gather(rounded, 'replica', axis=1, tiled=True)  106 us
    all_to_all x1, local copies, waits for them, and re-layouts, on_device(): lax.all_to_all(local, 'fsdp', split_axis=2, concat_axis=1, tiled=True)  60.3 us
    all_to_all x2, local copies, waits for them, and re-layouts, on_device(): lax.all_to_all(copies, 'fsdp', split_axis=1, concat_axis=2, tiled=True)  48.4 us
    unnamed x5, local copies, waits for them, and re-layouts  47 us
  transfers between devices with their start and end apart: 2, of which 2 were waited for; matrix products, arithmetic and copies ran while one was open for 0% of the time, Pallas kernels for 0%

commit v1 on v0

--- a/solution.py
+++ b/solution.py
@@ -15,7 +15,18 @@
     velocity = 0.9 * momentum + outer
     updated = master - 0.7 * (outer + 0.9 * velocity)
     rounded = updated.astype(jnp.bfloat16)
-    copies = lax.all_gather(rounded, "replica", axis=1, tiled=True)
+    axis_total = lax.axis_size("replica")
+    carry_in = sorted(((b, (b + 1) % axis_total) for b in range(axis_total)))
+    aux = rounded
+    gallery = [aux]
+    i = 1
+    while i < axis_total:
+        aux = lax.ppermute(aux, "replica", carry_in)
+        gallery.insert(0, aux)
+        i += 1
+    passed = jnp.concatenate(gallery, axis=1)
+    v_now = lax.axis_index("replica")
+    copies = jnp.roll(passed, (v_now + 1) * rounded.shape[1], axis=1)
     spread = lax.all_to_all(copies, "fsdp", split_axis=1, concat_axis=2, tiled=True)
     return (updated, velocity, spread)
 

time: 1330 us -> 1450 us (1.090)
  local copies, waits for them, and re-layouts: 164 us -> 246 us
  waiting for transfers between devices: 392 us -> 430 us
    ppermute x0 -> x3, waiting for transfers between devices: none -> 144 us  [on_device(): aux = lax.ppermute(aux, 'replica', carry_in)]
    all_gather x1 -> x0, waiting for transfers between devices: 106 us -> none  [on_device(): copies = lax.all_gather(rounded, 'replica', axis=1, tiled=True)]
    dynamic_slice x0 -> x2, local copies, waits for them, and re-layouts: none -> 57.4 us  [on_device(): copies = jnp.roll(passed, (v_now + 1) * rounded.shape[1], axis=1)]
    unnamed x5 -> x20, local copies, waits for them, and re-layouts: 47 us -> 77.6 us
    unnamed x3 -> x2, waiting for transfers between devices: 286 us -> 286 us
  transfers between devices with their start and end apart: 2 -> 4, of which waited for: 2 -> 4; matrix products, arithmetic and copies ran while one was open for 0% -> 0% of each run, Pallas kernels for 0% -> 0%
where the time goes in v1:
time: 1450 us; the launch traced here: 1440 us
  blocking collectives  739 us (51%)
  waiting for transfers between devices  430 us (30%)
  local copies, waits for them, and re-layouts  246 us (17%)
  between operations  14.7 us (1%)
    all_to_all x1, blocking collectives, on_device(): lax.all_to_all(local, 'fsdp', split_axis=2, concat_axis=1, tiled=True)  372 us
    all_to_all x1, blocking collectives, on_device(): lax.all_to_all(copies, 'fsdp', split_axis=1, concat_axis=2, tiled=True)  367 us
    unnamed x2, waiting for transfers between devices  286 us
    ppermute x3, waiting for transfers between devices, on_device(): aux = lax.ppermute(aux, 'replica', carry_in)  144 us
    unnamed x20, local copies, waits for them, and re-layouts  77.6 us
    all_to_all x1, local copies, waits for them, and re-layouts, on_device(): lax.all_to_all(local, 'fsdp', split_axis=2, concat_axis=1, tiled=True)  60.3 us
    dynamic_slice x2, local copies, waits for them, and re-layouts, on_device(): copies = jnp.roll(passed, (v_now + 1) * rounded.shape[1], axis=1)  57.4 us
    all_to_all x2, local copies, waits for them, and re-layouts, on_device(): lax.all_to_all(copies, 'fsdp', split_axis=1, concat_axis=2, tiled=True)  48.4 us
  transfers between devices with their start and end apart: 4, of which 4 were waited for; matrix products, arithmetic and copies ran while one was open for 0% of the time, Pallas kernels for 0%

profile of v1, /device:TPU:0, one launch (start us, length us, event | category | flops | bytes accessed | tf_op | source)
XLA Modules:
  0.0 1441.9 jit_solution(3672924209705845874)
XLA Ops:
  7.2 0.0 all-reduce.3.cloned.1.call-start
  7.2 40.8 %copy.40 = bf16[1,2,256,16384]{2,1,3,0:T(2,128)(2,1)} copy(bf16[1,2,256,16384]{3,2,1,0:T(8,128)(2,1)} %param.3) | data formatting | bytes 33554432 | tf_op args[0]
  48.0 372.0 %all_to_all.36 = bf16[2,256,16384]{1,0,2:T(2,128)(2,1)} all-to-all(bf16[2,256,16384]{1,0,2:T(2,128)(2,1)} %bitcast.14), channel_id=1, replica_groups=mesh['replica'=4,'fsdp'=8] {'fsdp'}, dimensions={2} | all-to-all | bytes 33554432 | tf_op jit(solution)/shard_map/all_to_all | solution.py:10
  420.0 60.3 %copy.41 = bf16[2,8,256,2048]{3,0,2,1:T(2,128)(2,1)} copy(bf16[2,8,256,2048]{2,0,3,1:T(2,128)(2,1)} %bitcast.12) | data formatting | bytes 33554432 | tf_op jit(solution)/shard_map/all_to_all | solution.py:10
  480.4 0.0 copy-start.4
  480.4 0.0 all-reduce.3.cloned.1.call-update
  480.4 0.6 copy-done.4
  481.0 0.6 dynamic-slice
  482.2 285.6 %all-reduce.3.cloned.1.call-done = bf16[2,2048,2048]{2,0,1:T(2,128)(2,1)} async-done(((bf16[2,2048,2048]{2,0,1:T(2,128)(2,1)}), bf16[2,2048,2048]{2,0,1:T(2,128)(2,1)}) %all-reduce.3.cloned.1.call-update) | async-done | bytes 16777232
  767.9 5.1 constant_dynamic-slice_fusion
  773.0 12.5 fusion
  785.5 0.0 copy-start
  785.5 1.9 copy-done
  787.4 0.0 collective-permute-start
  787.4 47.9 %collective-permute-done = bf16[2,512,2048]{2,1,0:T(8,128)(2,1)S(1)} collective-permute-done((bf16[2,512,2048]{2,1,0:T(8,128)(2,1)S(1)}, bf16[2,512,2048]{2,1,0:T(8,128)(2,1)S(1)}, u32[]{:S(2)}, u32[]{:S(2)}) %collective-permute-start) | collective-permute-done | bytes 4194336 | tf_op jit(solution)/shard_map/ppermute | solution.py:24
  835.4 0.0 copy-start.2
  835.4 2.0 copy-done.2
  837.4 0.0 collective-permute-start.1
  837.4 48.0 %collective-permute-done.1 = bf16[2,512,2048]{2,1,0:T(8,128)(2,1)} collective-permute-done((bf16[2,512,2048]{2,1,0:T(8,128)(2,1)S(1)}, bf16[2,512,2048]{2,1,0:T(8,128)(2,1)}, u32[]{:S(2)}, u32[]{:S(2)}) %collective-permute-start.1) | collective-permute-done | bytes 4194336 | tf_op jit(solution)/shard_map/ppermute | solution.py:24
  885.4 0.0 collective-permute-start.2
  885.4 0.0 copy-start.3
  885.4 0.0 copy-start.1
  885.4 48.2 %collective-permute-done.2 = bf16[2,512,2048]{2,1,0:T(8,128)(2,1)} collective-permute-done((bf16[2,512,2048]{2,1,0:T(8,128)(2,1)}, bf16[2,512,2048]{2,1,0:T(8,128)(2,1)}, u32[]{:S(2)}, u32[]{:S(2)}) %collective-permute-start.2) | collective-permute-done | bytes 4194336 | tf_op jit(solution)/shard_map/ppermute | solution.py:24
  933.7 4.9 constant_dynamic-update-slice_fusion.7
  938.5 4.8 constant_dynamic-update-slice_fusion.6
  943.4 0.0 copy-done.3
  943.4 2.4 constant_dynamic-update-slice_fusion.5
  945.7 0.0 copy-done.1
  945.7 2.4 constant_dynamic-update-slice_fusion.4
  948.2 4.9 constant_dynamic-update-slice_fusion.3
  953.1 4.8 constant_dynamic-update-slice_fusion.2
  957.9 2.4 constant_dynamic-update-slice_fusion.1
  960.3 2.3 constant_dynamic-update-slice_fusion
  962.5 8.5 constant_dynamic-slice_fusion.1
  971.1 48.9 %copy.43 = bf16[2,2048,2048]{2,0,1:T(2,128)(2,1)} copy(bf16[2,2048,2048]{2,1,0:T(8,128)(2,1)S(1)} %constant_dynamic-slice_fusion.1) | data formatting | bytes 33554432 | tf_op jit(solution)/shard_map/jit(_roll_dynamic)/dynamic_slice | solution.py:29
  1019.9 366.7 %all_to_all.37 = bf16[2,2048,2048]{2,0,1:T(2,128)(2,1)S(1)} all-to-all(bf16[2,2048,2048]{2,0,1:T(2,128)(2,1)} %copy.43), channel_id=1, replica_groups=mesh['replica'=4,'fsdp'=8] {'fsdp'}, dimensions={1} | all-to-all | bytes 33554432 | tf_op jit(solution)/shard_map/all_to_all | solution.py:30
  1386.6 22.9 %copy.44 = bf16[2,256,8,2048]{3,2,1,0:T(8,128)(2,1)} copy(bf16[2,256,8,2048]{3,0,1,2:T(2,128)(2,1)S(1)} %bitcast.13) | data formatting | bytes 33554432 | tf_op jit(solution)/shard_map/all_to_all | solution.py:30
  1409.5 25.5 %all_to_all.33 = bf16[2,256,16384]{2,1,0:T(8,128)(2,1)} reshape(bf16[2,256,8,2048]{3,2,1,0:T(8,128)(2,1)} %copy.44) | data formatting | bytes 33554432 | tf_op jit(solution)/shard_map/all_to_all | solution.py:30
Async XLA Ops:
  7.2 760.7 %all-reduce.3.cloned.1.call-start = ((), (), s32[]{:S(2)}) async-start(), calls=%async_computation.2 | async-start | bytes 33554432
  480.4 0.7 copy-start.4
  785.5 1.9 copy-start
  787.4 47.9 %collective-permute-start = (bf16[2,512,2048]{2,1,0:T(8,128)(2,1)S(1)}, bf16[2,512,2048]{2,1,0:T(8,128)(2,1)S(1)}, u32[]{:S(2)}, u32[]{:S(2)}) collective-permute-start(bf16[2,512,2048]{2,1,0:T(8,128)(2,1)S(1)} %get-tuple-element.12), channel_id=1, source_target_pairs={{0,8},{8,16},{16,24},{24,0},{1,9},{9,17},{17,25},{25,1},{2,10},{10... | collective-permute-start | bytes 12582920 | tf_op jit(solution)/shard_map/ppermute | solution.py:24
  835.4 2.0 copy-start.2
  837.4 48.0 %collective-permute-start.1 = (bf16[2,512,2048]{2,1,0:T(8,128)(2,1)S(1)}, bf16[2,512,2048]{2,1,0:T(8,128)(2,1)}, u32[]{:S(2)}, u32[]{:S(2)}) collective-permute-start(bf16[2,512,2048]{2,1,0:T(8,128)(2,1)S(1)} %collective-permute-done), channel_id=1, source_target_pairs={{0,8},{8,16},{16,24},{24,0},{1,9},{9,17},{17,25},{25,1},{2,10},{10... | collective-permute-start | bytes 12582920 | tf_op jit(solution)/shard_map/ppermute | solution.py:24
  885.4 48.2 %collective-permute-start.2 = (bf16[2,512,2048]{2,1,0:T(8,128)(2,1)}, bf16[2,512,2048]{2,1,0:T(8,128)(2,1)}, u32[]{:S(2)}, u32[]{:S(2)}) collective-permute-start(bf16[2,512,2048]{2,1,0:T(8,128)(2,1)} %collective-permute-done.1), channel_id=1, source_target_pairs={{0,8},{8,16},{16,24},{24,0},{1,9},{9,17},{17,25},{25,1},{2,10},{10... | collective-permute-start | bytes 12582920 | tf_op jit(solution)/shard_map/ppermute | solution.py:24
  885.4 57.9 %copy-start.3 = (bf16[2,512,2048]{2,1,0:T(8,128)(2,1)S(1)}, bf16[2,512,2048]{2,1,0:T(8,128)(2,1)}, u32[]{:S(2)}) copy-start(bf16[2,512,2048]{2,1,0:T(8,128)(2,1)} %copy-done.2) | copy-start | bytes 12582916
  885.4 60.3 %copy-start.1 = (bf16[2,512,2048]{2,1,0:T(8,128)(2,1)S(1)}, bf16[2,512,2048]{2,1,0:T(8,128)(2,1)}, u32[]{:S(2)}) copy-start(bf16[2,512,2048]{2,1,0:T(8,128)(2,1)} %copy-done) | copy-start | bytes 12582916
Sparse Core Ops, SparseCore 0:
  480.5 287.3 all-reduce.2
